TPU v7x, 32 devices: a whole 2x2x4 slice. The times are simulated.
32 devices in a mesh: obs: 2 (over y), bt: 4 (over z), freq: 2 (over x), pol: 2 (over core).
Axes of the slice: x: 2, y: 2, z: 4, core: 2. Of those that a mesh axis runs over, the one named last changes fastest.
Arguments:
- gains: float32 [16, 4, 8, 1984], P(('obs', 'bt', 'pol'), 'freq'), parts along dimension 0, may hold values from -3 to 3
- visibilities: bfloat16 [16, 4, 8, 4096], P('obs', 'freq', None, ('bt', 'pol')), parts along dimension 0, may hold values from -6 to 6
- first_station: int32 [8192], P(('obs', 'bt', 'pol')), parts along dimension 0, may hold values from 0 to 61
- second_station: int32 [8192], P(('obs', 'bt', 'pol')), parts along dimension 0, may hold values from 0 to 61, as said below
- filled_row_count: int32 [16], P(('obs', 'bt', 'pol')), parts along dimension 0, may hold values from 256 to 512
- facet_dir: int32 [16], P('obs'), parts along dimension 0, may hold values from 0 to 7, each once
Outputs:
- corrected: bfloat16 [16, 4, 8, 4096], P('obs', 'freq', None, ('bt', 'pol')), parts along dimension 0
There are 2 independent parts, one for each index of `obs`. A program takes and returns all parts, laid end to end along the dimension named above; each array names one. Nothing has to cross between parts.
Inputs may be any that keep to these rules, and one draw needn't show every extreme that they name: In every row second_station differs from first_station. `facet_dir`: each direction names exactly one facet.
All inputs are finite; a program needn't handle non-finite values.
Results may differ from a plain program's by a relative error of at most 0.001.
Values sent between devices are 32-bit elements; how exact they have to be, the bound alone decides.
No kernel may reach another device: no remote copies, remote signals or barrier semaphores. Data moves between devices by JAX's collectives and lax.ppermute only.
A program may use at most 64 MiB of HBM per device.

v0:
```python
import jax
import jax.numpy as jnp
from jax import lax
from jax.sharding import PartitionSpec as P

ARRAY_STATIONS = 62
GAIN_SLOT_COUNT = 4


def entry(values, row_at, col_at):
    return (values[..., 2 * row_at + col_at, :], values[..., 4 + 2 * row_at + col_at, :])


def apply_jones(left_matrix, data, right_matrix):
    real_parts = []
    imag_parts = []
    for out_row in (0, 1):
        for out_col in (0, 1):
            total_re = jnp.zeros_like(left_matrix[..., 0, :])
            total_im = jnp.zeros_like(left_matrix[..., 0, :])
            for middle in (0, 1):
                for column in (0, 1):
                    left_re, left_im = entry(left_matrix, out_row, middle)
                    data_re, data_im = entry(data, middle, column)
                    right_re, right_im = entry(right_matrix, out_col, column)
                    prod_re = left_re * data_re - left_im * data_im
                    prod_im = left_re * data_im + left_im * data_re
                    total_re = total_re + prod_re * right_re + prod_im * right_im
                    total_im = total_im + prod_im * right_re - prod_re * right_im
            real_parts.append(total_re)
            imag_parts.append(total_im)
    return jnp.stack(real_parts + imag_parts, axis=-2)


def expand_slots(gain_window, antenna, block_rows, slots, stations):
    facets, chans, comps, _ = gain_window.shape
    current = gain_window[..., : slots * stations].reshape(facets, chans, comps, slots, stations)
    following = gain_window[..., stations:].reshape(facets, chans, comps, slots, stations)
    paired = jnp.concatenate([current, following], axis=4)
    per_slot = block_rows // slots
    grouped = antenna.reshape(slots, per_slot)
    fraction = (jnp.arange(per_slot, dtype=jnp.int32).astype(jnp.float32) + 0.5) / per_slot
    station_ids = jnp.arange(stations, dtype=jnp.int32)
    station_mask = (station_ids[None, :, None] == grouped[:, None, :]).astype(jnp.float32)
    table = jnp.concatenate([station_mask * (1.0 - fraction), station_mask * fraction], axis=1)
    spread = jnp.einsum("fckjn,jnp->fckjp", paired, table, precision=lax.Precision.HIGHEST)
    return spread.reshape(facets, chans, comps, block_rows)


def apply_correction(
    gain_window, block_visibilities, first_station_gain, second_station_gain, filled_rows
):
    block_rows = block_visibilities.shape[3]
    left_matrix = expand_slots(
        gain_window, first_station_gain, block_rows, GAIN_SLOT_COUNT, ARRAY_STATIONS
    )
    right_matrix = expand_slots(
        gain_window, second_station_gain, block_rows, GAIN_SLOT_COUNT, ARRAY_STATIONS
    )
    product = apply_jones(left_matrix, block_visibilities.astype(jnp.float32), right_matrix)
    live_mask = jnp.arange(block_rows, dtype=jnp.int32) < filled_rows
    return jnp.where(live_mask, product, 0.0 * product).astype(jnp.bfloat16)


def relay(payload):
    relaid = lax.all_to_all(payload, ("bt", "pol"), split_axis=3, concat_axis=0, tiled=True)
    return relaid


def select_facets(relaid, facet_dir):
    directions = relaid.shape[0]
    onehot = (facet_dir[:, None] == jnp.arange(directions, dtype=jnp.int32)[None, :]).astype(
        jnp.float32
    )
    return jnp.einsum("fd,dckn->fckn", onehot, relaid, precision=lax.Precision.HIGHEST)


def shards(gains, visibilities, first_station, second_station, filled_row_count, facet_dir):
    block_count = lax.axis_size(("bt", "pol"))
    dirs_here, chans_here, comps, _ = gains.shape
    by_slot = gains.reshape(
        dirs_here, chans_here, comps, block_count, GAIN_SLOT_COUNT, ARRAY_STATIONS
    )
    firsts = by_slot[:, :, :, :, 0, :]
    final_one = by_slot[:, :, :, block_count - 1 :, GAIN_SLOT_COUNT - 1, :]
    nexts = jnp.concatenate([firsts[:, :, :, 1:, :], final_one], axis=3)
    own_slots = by_slot.reshape(
        dirs_here, chans_here, comps, block_count, GAIN_SLOT_COUNT * ARRAY_STATIONS
    )
    windows = jnp.concatenate([own_slots, nexts], axis=4)
    windows = windows.reshape(
        dirs_here, chans_here, comps, block_count * (GAIN_SLOT_COUNT + 1) * ARRAY_STATIONS
    )
    gain_window = select_facets(relay(windows), facet_dir)
    return apply_correction(
        gain_window, visibilities, first_station, second_station, filled_row_count[0]
    )


def solution(mesh):
    return jax.shard_map(
        shards,
        mesh=mesh,
        in_specs=(
            P(("obs", "bt", "pol"), "freq", None, None),
            P("obs", "freq", None, ("bt", "pol")),
            P(("obs", "bt", "pol")),
            P(("obs", "bt", "pol")),
            P(("obs", "bt", "pol")),
            P("obs"),
        ),
        out_specs=P("obs", "freq", None, ("bt", "pol")),
        check_vma=False,
    )
```

profile of v0, /device:TPU:0, one launch (start us, length us, event | category | flops | bytes accessed | tf_op | source)
XLA Modules:
  0.0 31.5 jit_solution(10585168810742284929)
XLA Ops:
  0.0 1.3 %reshape.32 = f32[1,2,8,8,4,62]{5,4,3,2,1,0:T(4,128)S(1)} reshape(f32[1,2,8,1984]{3,2,1,0:T(8,128)} %param.6) | data formatting | bytes 253952 | tf_op jit(solution)/shard_map/reshape | solution.py:81
  1.4 1.0 %reshape_reshape.3 = f32[1,2,8,8,248]{4,3,2,1,0:T(8,128)S(1)} reshape(f32[1,2,8,1984]{3,2,1,0:T(8,128)} %param.6) | data formatting | bytes 253952 | tf_op jit(solution)/shard_map/reshape;reshape | solution.py:87
  2.4 0.1 maximum_maximum_fusion
  2.6 0.0 copy-start
  2.6 0.0 copy-start.1
  2.6 0.0 copy-start.2
  2.6 2.2 %copy.38 = f32[1,2,8,8,310]{2,1,4,3,0:T(2,128)S(1)} copy(f32[1,2,8,8,310]{4,3,2,1,0:T(8,128)S(1)} %maximum_maximum_fusion) | data formatting | bytes 317440 | tf_op jit(solution)/shard_map/concatenate | solution.py:90
  4.8 4.0 %reshape.41 = f32[8,1,4960]{2,1,0:T(1,128)} reshape(f32[2480,1,2,8]{3,2,1,0:T(2,128)S(1)} %bitcast.55) | data formatting | bytes 317440
  8.8 6.4 %all-to-all-start = ((f32[8,1,4960]{2,1,0:T(1,128)}), f32[8,1,4960]{2,1,0:T(1,128)S(1)}, u32[]{:S(2)}, u32[]{:S(2)}) async-start(f32[8,1,4960]{2,1,0:T(1,128)} %reshape.41), calls=%async_computation | async-start | bytes 319488 | tf_op jit(solution)/shard_map/all_to_all | solution.py:66
  15.1 0.0 copy-done
  15.2 0.1 copy_convert_fusion
  15.9 0.0 copy-done.1
  15.9 0.0 copy-done.2
  16.0 6.3 %all-to-all-done = f32[8,1,4960]{2,1,0:T(1,128)S(1)} async-done(((f32[8,1,4960]{2,1,0:T(1,128)}), f32[8,1,4960]{2,1,0:T(1,128)S(1)}, u32[]{:S(2)}, u32[]{:S(2)}) %all-to-all-start) | async-done | bytes 158752 | tf_op jit(solution)/shard_map/all_to_all | solution.py:66
  22.3 0.5 %broadcast.50 = f32[]{:T(128)} broadcast(f32[]{:T(128)} %constant.71), dimensions={} | broadcast | bytes 8 | tf_op jit(solution)/shard_map/all_to_all | solution.py:66
  22.8 1.0 %reduce = f32[8,4960]{1,0:T(8,128)S(1)} reduce(f32[8,1,4960]{2,1,0:T(1,128)S(1)} %all-to-all-done, f32[]{:T(128)} %broadcast.50), dimensions={1}, to_apply=%all_to_all.13.reduce_sub_computation | reduce | bytes 317444 | tf_op jit(solution)/shard_map/all_to_all | solution.py:66
  23.8 0.0 copy-start.3
  23.8 2.0 %reshape.42 = f32[2480,1,2,8]{3,2,1,0:T(2,128)S(1)} reshape(f32[8,4960]{1,0:T(8,128)S(1)} %reduce) | data formatting | bytes 317440
  25.8 2.1 %copy.65 = f32[1,2,8,8,310]{4,3,2,1,0:T(8,128)S(1)} copy(f32[1,2,8,8,310]{2,1,4,3,0:T(2,128)S(1)} %bitcast.56) | data formatting | bytes 317440 | tf_op jit(solution)/shard_map/all_to_all | solution.py:66
  27.9 0.0 copy-done.3
  27.9 0.3 fusion.5
  28.2 0.1 fusion.18
  28.3 0.2 reshape.34
  28.5 0.2 copy.40
  28.6 0.2 reshape.35
  28.8 0.2 copy.41
  29.0 0.4 %convolution_bitcast_fusion = f32[8,2,8,4,128]{4,2,1,0,3:T(8,128)S(1)} fusion(f32[4,62,128]{2,1,0:T(8,128)S(1)} %get-tuple-element.44, f32[4,62,128]{2,1,0:T(8,128)S(1)} %get-tuple-element.43, f32[8,2,8,4,62]{4,2,1,0,3:T(8,128)S(1)} %copy.41, f32[8,2,8,4,62]{4,2,1,0,3:T(8,128)S(1)} %copy.40), kind=kOutput, calls=%fused_computation | convolution fusion | flops 97644544 | bytes 770048 | tf_op jit(solution)/shard_map/fckjn,jnp->fckjp/dot_general | solution.py:46
  29.5 0.2 fusion.17
  29.6 0.4 %convolution_bitcast_fusion.1 = f32[8,2,8,4,128]{4,2,1,0,3:T(8,128)S(1)} fusion(f32[4,62,128]{2,1,0:T(8,128)S(1)} %get-tuple-element.45, f32[4,62,128]{2,1,0:T(8,128)S(1)} %get-tuple-element.46, f32[8,2,8,4,62]{4,2,1,0,3:T(8,128)S(1)} %copy.41, f32[8,2,8,4,62]{4,2,1,0,3:T(8,128)S(1)} %copy.40), kind=kOutput, calls=%fused_computation.1 | convolution fusion | flops 97644544 | bytes 770048 | tf_op jit(solution)/shard_map/fckjn,jnp->fckjp/dot_general | solution.py:46
  30.1 0.2 fusion.16
  30.3 0.1 add_dynamic-update-slice_fusion.3
  30.4 0.1 add_dynamic-update-slice_fusion.1
  30.8 0.7 %copy.61 = bf16[8,2,8,512]{3,2,1,0:T(8,128)(2,1)} copy(bf16[8,2,8,512]{3,0,2,1:T(8,128)(2,1)S(1)} %fusion) | data formatting | bytes 262144 | tf_op jit(solution)/shard_map/convert_element_type | solution.py:62
  (15 shorter events, 0.5 us)
Async XLA Ops:
  2.6 12.6 %copy-start = (bf16[8,2,8,512]{3,2,1,0:T(8,128)(2,1)S(1)}, bf16[8,2,8,512]{3,2,1,0:T(8,128)(2,1)}, u32[]{:S(2)}) copy-start(bf16[8,2,8,512]{3,2,1,0:T(8,128)(2,1)} %param.7) | copy-start | bytes 393220
  2.6 13.3 %copy-start.1 = (s32[512]{0:T(512)S(1)}, s32[512]{0:T(512)}, u32[]{:S(2)}) copy-start(s32[512]{0:T(512)} %param.9) | copy-start | bytes 6148
  2.6 13.3 %copy-start.2 = (s32[512]{0:T(512)S(1)}, s32[512]{0:T(512)}, u32[]{:S(2)}) copy-start(s32[512]{0:T(512)} %param.8) | copy-start | bytes 6148
  8.8 13.5 %all-to-all-start = ((f32[8,1,4960]{2,1,0:T(1,128)}), f32[8,1,4960]{2,1,0:T(1,128)S(1)}, u32[]{:S(2)}, u32[]{:S(2)}) async-start(f32[8,1,4960]{2,1,0:T(1,128)} %reshape.41), calls=%async_computation | async-start | bytes 319488 | tf_op jit(solution)/shard_map/all_to_all | solution.py:66
  23.8 4.1 %copy-start.3 = (s32[8]{0:T(128)S(1)}, s32[8]{0:T(128)}, u32[]{:S(2)}) copy-start(s32[8]{0:T(128)} %param.11) | copy-start | bytes 100
where the time goes:
time: 31.8 us; the launch traced here: 31.5 us
  local copies, waits for them, and re-layouts  15 us (47%)
  starting transfers between devices  6.35 us (20%)
  waiting for transfers between devices  6.29 us (20%)
  other arithmetic  1.77 us (6%)
  matrix products  1.16 us (4%)
  between operations  0.94 us (3%)
    all_to_all x1, starting transfers between devices, relay(): lax.all_to_all(payload, ('bt', 'pol'), split_axis=3, concat_axis=0, tiled...  6.35 us
    all_to_all x1, waiting for transfers between devices, relay(): lax.all_to_all(payload, ('bt', 'pol'), split_axis=3, concat_axis=0, tiled...  6.29 us
    unnamed x10, local copies, waits for them, and re-layouts  5.99 us
    all_to_all x2, local copies, waits for them, and re-layouts, relay(): lax.all_to_all(payload, ('bt', 'pol'), split_axis=3, concat_axis=0, tiled...  2.57 us
    concatenate x1, local copies, waits for them, and re-layouts, shards(): windows = jnp.concatenate([own_slots, nexts], axis=4)  2.18 us
    reshape x1, local copies, waits for them, and re-layouts, shards(): gains.reshape(dirs_here, chans_here, comps, block_count, GAIN_SLOT_COUNT,...  1.31 us
    another operation x1, local copies, waits for them, and re-layouts, shards(): by_slot.reshape(dirs_here, chans_here, comps, block_count, GAIN_SLOT_COUN...  1.03 us
    all_to_all x1, other arithmetic, relay(): lax.all_to_all(payload, ('bt', 'pol'), split_axis=3, concat_axis=0, tiled...  1.02 us
  transfers between devices with their start and end apart: 1, of which 1 were waited for; matrix products, arithmetic and copies ran while one was open for 0% of the time, Pallas kernels for 0%

commit v1 on v0

--- a/solution.py
+++ b/solution.py
@@ -5,6 +5,18 @@
 
 ARRAY_STATIONS = 62
 GAIN_SLOT_COUNT = 4
+
+
+def find_sheet(sample):
+    return jnp.concatenate(
+        lax.all_to_all(
+            jnp.stack(jnp.split(sample, lax.axis_size(("bt", "pol")), axis=3), axis=0),
+            ("bt", "pol"),
+            0,
+            0,
+        ),
+        axis=0,
+    )
 
 
 def entry(values, row_at, col_at):
@@ -63,7 +75,7 @@
 
 
 def relay(payload):
-    relaid = lax.all_to_all(payload, ("bt", "pol"), split_axis=3, concat_axis=0, tiled=True)
+    relaid = find_sheet(payload)
     return relaid
 
 

time: 31.8 us -> 26.7 us (0.84)
  local copies, waits for them, and re-layouts: 15 us -> 10.4 us
  other arithmetic: 1.77 us -> 0.75 us
  waiting for transfers between devices: 6.29 us -> 6.79 us
    all_to_all x2 -> x0, local copies, waits for them, and re-layouts: 2.57 us -> none  [relay(): lax.all_to_all(payload, ('bt', 'pol'), split_axis=3, concat_axis=0, tiled...]
    concatenate x1 -> x0, local copies, waits for them, and re-layouts: 2.18 us -> none  [shards(): windows = jnp.concatenate([own_slots, nexts], axis=4)]
    all_to_all x1 -> x0, other arithmetic: 1.02 us -> none  [relay(): lax.all_to_all(payload, ('bt', 'pol'), split_axis=3, concat_axis=0, tiled...]
    another operation x1, local copies, waits for them, and re-layouts: 1.03 us -> 0.12 us  [shards(): by_slot.reshape(dirs_here, chans_here, comps, block_count, GAIN_SLOT_COUN...]
    another operation x0 -> x1, local copies, waits for them, and re-layouts: none -> 0.67 us  [find_sheet(): jnp.stack(jnp.split(sample, lax.axis_size(('bt', 'pol')), axis=3), axis=0)]
    all_to_all x1, waiting for transfers between devices: 6.29 us -> 6.79 us  [find_sheet(): lax.all_to_all(jnp.stack(jnp.split(sample, lax.axis_size(('bt', 'pol')),...]
    unnamed x10 -> x17, local copies, waits for them, and re-layouts: 5.99 us -> 6.21 us
  transfers between devices with their start and end apart: 1 -> 1, of which waited for: 1 -> 1; matrix products, arithmetic and copies ran while one was open for 0% -> 1% of each run, Pallas kernels for 0% -> 0%
where the time goes in v1:
time: 26.7 us; the launch traced here: 26.4 us
  local copies, waits for them, and re-layouts  10.4 us (39%)
  waiting for transfers between devices  6.79 us (25%)
  starting transfers between devices  6.49 us (24%)
  matrix products  1.15 us (4%)
  between operations  0.9 us (3%)
  other arithmetic  0.75 us (3%)
    all_to_all x1, waiting for transfers between devices, find_sheet(): lax.all_to_all(jnp.stack(jnp.split(sample, lax.axis_size(('bt', 'pol')),...  6.79 us
    all_to_all x1, starting transfers between devices, find_sheet(): lax.all_to_all(jnp.stack(jnp.split(sample, lax.axis_size(('bt', 'pol')),...  6.49 us
    unnamed x17, local copies, waits for them, and re-layouts  6.21 us
    reshape x1, local copies, waits for them, and re-layouts, shards(): gains.reshape(dirs_here, chans_here, comps, block_count, GAIN_SLOT_COUNT,...  1.31 us
    dot_general x2, matrix products, expand_slots(): jnp.einsum('fckjn,jnp->fckjp', paired, table, precision=lax.Precision.HIG...  0.87 us
    convert_element_type x1, local copies, waits for them, and re-layouts, apply_correction(): return jnp.where(live_mask, product, 0.0 * product).astype(jnp.bfloat16)  0.7 us
    another operation x1, local copies, waits for them, and re-layouts, find_sheet(): jnp.stack(jnp.split(sample, lax.axis_size(('bt', 'pol')), axis=3), axis=0)  0.67 us
  transfers between devices with their start and end apart: 1, of which 1 were waited for; matrix products, arithmetic and copies ran while one was open for 1% of the time, Pallas kernels for 0%

profile of v1, /device:TPU:0, one launch (start us, length us, event | category | flops | bytes accessed | tf_op | source)
XLA Modules:
  0.0 26.4 jit_solution(16037608046344883767)
XLA Ops:
  0.0 1.3 %reshape.35 = f32[1,2,8,8,4,62]{5,4,3,2,1,0:T(4,128)S(1)} reshape(f32[1,2,8,1984]{3,2,1,0:T(8,128)} %param.6) | data formatting | bytes 253952 | tf_op jit(solution)/shard_map/reshape | solution.py:93
  1.3 0.0 copy-start
  1.4 0.8 %copy-done = f32[1,2,8,1984]{3,2,1,0:T(8,128)S(1)} copy-done((f32[1,2,8,1984]{3,2,1,0:T(8,128)S(1)}, f32[1,2,8,1984]{3,2,1,0:T(8,128)}, u32[]{:S(2)}) %copy-start) | copy-done | bytes 127000
  2.2 0.1 reshape_reshape.3
  2.4 0.1 maximum_maximum_fusion
  2.5 0.1 reshape.36
  2.6 0.6 %constant_dynamic-update-slice_fusion.7 = f32[8,1,2,8,310]{4,3,2,1,0:T(8,128)} fusion(f32[1,2,8,2480]{3,2,1,0:T(8,128)S(1)} %reshape.36), kind=kLoop, calls=%fused_computation.31 | loop fusion | bytes 44416
  3.2 0.7 %constant_dynamic-update-slice_fusion.6 = f32[8,1,2,8,310]{4,3,2,1,0:T(8,128)} fusion(f32[8,1,2,8,310]{4,3,2,1,0:T(8,128)} %constant_dynamic-update-slice_fusion.7, f32[1,2,8,2480]{3,2,1,0:T(8,128)S(1)} %reshape.36), kind=kLoop, calls=%fused_computation.30 | loop fusion | bytes 44416
  3.9 0.7 %constant_dynamic-update-slice_fusion.5 = f32[8,1,2,8,310]{4,3,2,1,0:T(8,128)} fusion(f32[8,1,2,8,310]{4,3,2,1,0:T(8,128)} %constant_dynamic-update-slice_fusion.6, f32[1,2,8,2480]{3,2,1,0:T(8,128)S(1)} %reshape.36), kind=kLoop, calls=%fused_computation.29 | loop fusion | bytes 44416
  4.6 0.7 %constant_dynamic-update-slice_fusion.4 = f32[8,1,2,8,310]{4,3,2,1,0:T(8,128)} fusion(f32[8,1,2,8,310]{4,3,2,1,0:T(8,128)} %constant_dynamic-update-slice_fusion.5, f32[1,2,8,2480]{3,2,1,0:T(8,128)S(1)} %reshape.36), kind=kLoop, calls=%fused_computation.28 | loop fusion | bytes 44416
  5.3 0.7 %constant_dynamic-update-slice_fusion.3 = f32[8,1,2,8,310]{4,3,2,1,0:T(8,128)} fusion(f32[8,1,2,8,310]{4,3,2,1,0:T(8,128)} %constant_dynamic-update-slice_fusion.4, f32[1,2,8,2480]{3,2,1,0:T(8,128)S(1)} %reshape.36), kind=kLoop, calls=%fused_computation.27 | loop fusion | bytes 44416
  6.0 0.7 %constant_dynamic-update-slice_fusion.2 = f32[8,1,2,8,310]{4,3,2,1,0:T(8,128)} fusion(f32[8,1,2,8,310]{4,3,2,1,0:T(8,128)} %constant_dynamic-update-slice_fusion.3, f32[1,2,8,2480]{3,2,1,0:T(8,128)S(1)} %reshape.36), kind=kLoop, calls=%fused_computation.26 | loop fusion | bytes 44416
  6.7 0.7 %constant_dynamic-update-slice_fusion.1 = f32[8,1,2,8,310]{4,3,2,1,0:T(8,128)} fusion(f32[8,1,2,8,310]{4,3,2,1,0:T(8,128)} %constant_dynamic-update-slice_fusion.2, f32[1,2,8,2480]{3,2,1,0:T(8,128)S(1)} %reshape.36), kind=kLoop, calls=%fused_computation.25 | loop fusion | bytes 44416
  7.3 0.7 %constant_dynamic-update-slice_fusion = f32[8,1,2,8,310]{4,3,2,1,0:T(8,128)} fusion(f32[8,1,2,8,310]{4,3,2,1,0:T(8,128)} %constant_dynamic-update-slice_fusion.1, f32[1,2,8,2480]{3,2,1,0:T(8,128)S(1)} %reshape.36), kind=kLoop, calls=%fused_computation.24 | loop fusion | bytes 44416 | tf_op jit(solution)/shard_map/stack | solution.py:13
  8.0 0.0 copy-start.1
  8.0 6.5 %all-to-all-start = ((f32[8,1,2,8,310]{4,3,2,1,0:T(8,128)}), f32[8,1,2,8,310]{4,3,2,1,0:T(8,128)S(1)}, u32[]{:S(2)}, u32[]{:S(2)}) async-start(f32[8,1,2,8,310]{4,3,2,1,0:T(8,128)} %constant_dynamic-update-slice_fusion), calls=%async_computation | async-start | bytes 393216 | tf_op jit(solution)/shard_map/all_to_all | solution.py:12
  14.5 0.0 copy-done.1
  14.5 0.1 copy_convert_fusion
  15.3 0.0 copy-start.3
  15.3 0.0 copy-start.2
  15.3 0.7 %copy-done.3 = s32[512]{0:T(512)S(1)} copy-done((s32[512]{0:T(512)S(1)}, s32[512]{0:T(512)}, u32[]{:S(2)}) %copy-start.3) | copy-done | bytes 2072
  15.9 0.0 copy-done.2
  16.0 0.0 copy-start.4
  16.0 6.8 %all-to-all-done = f32[8,1,2,8,310]{4,3,2,1,0:T(8,128)S(1)} async-done(((f32[8,1,2,8,310]{4,3,2,1,0:T(8,128)}), f32[8,1,2,8,310]{4,3,2,1,0:T(8,128)S(1)}, u32[]{:S(2)}, u32[]{:S(2)}) %all-to-all-start) | async-done | bytes 158752 | tf_op jit(solution)/shard_map/all_to_all | solution.py:12
  22.8 0.0 copy-done.4
  22.8 0.3 %fusion.5 = f32[8,2,8,310]{3,0,2,1:T(8,128)S(1)} fusion(f32[8,1,2,8,310]{4,3,2,1,0:T(8,128)S(1)} %all-to-all-done, s32[8]{0:T(128)S(1)} %copy-done.4), kind=kOutput, calls=%fused_computation.14 | convolution fusion | flops 3809344 | bytes 317472 | tf_op jit(solution)/shard_map/fd,dckn->fckn/dot_general | solution.py:87
  23.1 0.1 fusion.19
  23.2 0.2 reshape.38
  23.4 0.2 copy.27
  23.5 0.2 reshape.39
  23.7 0.2 copy.28
  23.9 0.4 %convolution_bitcast_fusion.1 = f32[8,2,8,4,128]{4,2,1,0,3:T(8,128)S(1)} fusion(f32[4,62,128]{2,1,0:T(8,128)S(1)} %get-tuple-element.45, f32[4,62,128]{2,1,0:T(8,128)S(1)} %get-tuple-element.46, f32[8,2,8,4,62]{4,2,1,0,3:T(8,128)S(1)} %copy.28, f32[8,2,8,4,62]{4,2,1,0,3:T(8,128)S(1)} %copy.27), kind=kOutput, calls=%fused_computation.1 | convolution fusion | flops 97644544 | bytes 770048 | tf_op jit(solution)/shard_map/fckjn,jnp->fckjp/dot_general | solution.py:58
  24.4 0.2 fusion.17
  24.5 0.4 %convolution_bitcast_fusion = f32[8,2,8,4,128]{4,2,1,0,3:T(8,128)S(1)} fusion(f32[4,62,128]{2,1,0:T(8,128)S(1)} %get-tuple-element.44, f32[4,62,128]{2,1,0:T(8,128)S(1)} %get-tuple-element.43, f32[8,2,8,4,62]{4,2,1,0,3:T(8,128)S(1)} %copy.28, f32[8,2,8,4,62]{4,2,1,0,3:T(8,128)S(1)} %copy.27), kind=kOutput, calls=%fused_computation | convolution fusion | flops 97644544 | bytes 770048 | tf_op jit(solution)/shard_map/fckjn,jnp->fckjp/dot_general | solution.py:58
  25.0 0.2 fusion.18
  25.2 0.1 constant_dynamic-update-slice_fusion.15
  25.3 0.1 constant_dynamic-update-slice_fusion.13
  25.7 0.7 %copy.48 = bf16[8,2,8,512]{3,2,1,0:T(8,128)(2,1)} copy(bf16[8,2,8,512]{3,0,2,1:T(8,128)(2,1)S(1)} %fusion) | data formatting | bytes 262144 | tf_op jit(solution)/shard_map/convert_element_type | solution.py:74
  (15 shorter events, 0.5 us)
Async XLA Ops:
  1.3 0.9 %copy-start = (f32[1,2,8,1984]{3,2,1,0:T(8,128)S(1)}, f32[1,2,8,1984]{3,2,1,0:T(8,128)}, u32[]{:S(2)}) copy-start(f32[1,2,8,1984]{3,2,1,0:T(8,128)} %param.6) | copy-start | bytes 380932
  8.0 6.5 %copy-start.1 = (bf16[8,2,8,512]{3,2,1,0:T(8,128)(2,1)S(1)}, bf16[8,2,8,512]{3,2,1,0:T(8,128)(2,1)}, u32[]{:S(2)}) copy-start(bf16[8,2,8,512]{3,2,1,0:T(8,128)(2,1)} %param.7) | copy-start | bytes 393220
  8.0 14.8 %all-to-all-start = ((f32[8,1,2,8,310]{4,3,2,1,0:T(8,128)}), f32[8,1,2,8,310]{4,3,2,1,0:T(8,128)S(1)}, u32[]{:S(2)}, u32[]{:S(2)}) async-start(f32[8,1,2,8,310]{4,3,2,1,0:T(8,128)} %constant_dynamic-update-slice_fusion), calls=%async_computation | async-start | bytes 393216 | tf_op jit(solution)/shard_map/all_to_all | solution.py:12
  15.3 0.7 %copy-start.3 = (s32[512]{0:T(512)S(1)}, s32[512]{0:T(512)}, u32[]{:S(2)}) copy-start(s32[512]{0:T(512)} %param.8) | copy-start | bytes 6148
  15.3 0.7 %copy-start.2 = (s32[512]{0:T(512)S(1)}, s32[512]{0:T(512)}, u32[]{:S(2)}) copy-start(s32[512]{0:T(512)} %param.9) | copy-start | bytes 6148
  16.0 6.8 %copy-start.4 = (s32[8]{0:T(128)S(1)}, s32[8]{0:T(128)}, u32[]{:S(2)}) copy-start(s32[8]{0:T(128)} %param.11) | copy-start | bytes 100
